TPU v7x, 32 devices: a whole 2x2x4 slice. The times are simulated.
32 devices in a mesh: dp: 8 (over y, x, core), mp: 4 (over z).
Axes of the slice: x: 2, y: 2, z: 4, core: 2. Of those that a mesh axis runs over, the one named last changes fastest.
Arguments:
- image_tokens: bfloat16 [128, 32, 1152], P('dp'), may hold values from -6 to 6
- image_counts: int32 [8, 4], P('dp'), may hold values from 2 to 4, as said below
- image_ids: int32 [128], P('dp'), may hold values from 0 to 31
- norm_gain: float32 [1152], replicated, may hold values from 0.1 to 1.9
- norm_bias: float32 [1152], replicated, may hold values from -3 to 3
- up_weight: bfloat16 [1152, 3072], P(None, 'mp'), may hold values from -0.1875 to 0.1875
- down_weight: bfloat16 [3072, 1152], P('mp'), may hold values from -0.109375 to 0.109375
- text_rows: bfloat16 [128, 1152], P(('dp', 'mp')), may hold values from -6 to 6
- text_counts: int32 [32], P(('dp', 'mp')), may hold values from 2 to 4, as said below
- text_ids: int32 [128], replicated, may hold values from 0 to 31
- logit_scale: float32 [1], replicated, may hold values from 30 to 45
- logit_bias: float32 [1], replicated, may hold values from -8 to -5.5
Outputs:
- text_grad: float32 [128, 1152], P(('dp', 'mp'))
Inputs may be any that keep to these rules, and one draw needn't show every extreme that they name: `image_counts`: entries count the valid rows among the 4 padded rows of one device's block; in every draw some block has all 4 rows valid. `text_counts`: entries count the valid rows among the 4 padded rows of one device's block; in every draw some block has all 4 rows valid.
All inputs are finite; a program needn't handle non-finite values.
Results may differ from a plain program's by a relative error of at most 0.02.
Values may be sent and summed in bfloat16 or wider, within the bound.
A program may use at most 64 MiB of HBM per device.

v0:
```python
import jax
import jax.numpy as jnp
from jax import lax
from jax.sharding import PartitionSpec as P

norm_eps = 1e-06


def from_behind(block, axis, distance):
    devices = range(lax.axis_size(axis))
    route = [((i - distance) % len(devices), i) for i in devices]
    return lax.ppermute(block, axis, route)


def layer_norm(row_values, gain_row, shift_row):
    values = row_values.astype(jnp.float32)
    center = jnp.mean(values, axis=-1, keepdims=True)
    spread = jnp.mean(jnp.square(values - center), axis=-1, keepdims=True)
    return (values - center) * lax.rsqrt(spread + norm_eps) * gain_row + shift_row


def unit_rows(values):
    return values * lax.rsqrt(jnp.sum(values * values, axis=-1, keepdims=True) + norm_eps)


def pair_terms(text_block, block_ids, image_emb, image_ids, image_valid, logit_mul, logit_add):
    cosines = lax.dot_general(
        text_block, image_emb, (((1,), (1,)), ((), ())), preferred_element_type=jnp.float32
    )
    logits = logit_mul * cosines + logit_add
    sign_table = jnp.where(block_ids[:, None] == image_ids[None, :], 1.0, -1.0).astype(jnp.float32)
    margin = -sign_table * logits
    weights = (image_valid[None, :] * -sign_table * jax.nn.sigmoid(margin) * logit_mul).astype(
        jnp.bfloat16
    )
    return jnp.dot(weights, image_emb, preferred_element_type=jnp.float32)


def local(
    image_tokens,
    image_counts,
    image_ids,
    norm_gain,
    norm_bias,
    up_weight,
    down_weight,
    text_rows,
    text_counts,
    text_ids,
    logit_scale,
    logit_bias,
):
    width_shards = lax.axis_size("mp")
    data_shards = lax.axis_size("dp")
    width_index = lax.axis_index("mp")
    data_index = lax.axis_index("dp")
    rows_dev = text_rows.shape[0]
    group_rows = image_tokens.shape[0]
    normed = layer_norm(image_tokens, norm_gain, norm_bias).astype(jnp.bfloat16)
    hidden = jax.nn.gelu(jnp.dot(normed, up_weight, preferred_element_type=jnp.float32)).astype(
        jnp.bfloat16
    )
    pooled_hidden = jnp.mean(hidden.astype(jnp.float32), axis=1).astype(jnp.bfloat16)
    partial_value = jnp.dot(pooled_hidden, down_weight, preferred_element_type=jnp.float32)
    pooled_tokens = jnp.mean(image_tokens.astype(jnp.float32), axis=1)
    tower_out = pooled_tokens + lax.psum(partial_value.astype(jnp.bfloat16), "mp").astype(
        jnp.float32
    )
    image_emb = unit_rows(tower_out).astype(jnp.bfloat16)
    slot_index = jnp.arange(group_rows, dtype=jnp.int32) % rows_dev
    image_valid = (
        slot_index < jnp.repeat(image_counts[0], rows_dev, total_repeat_length=group_rows)
    ).astype(jnp.float32)
    text_valid = (jnp.arange(rows_dev, dtype=jnp.int32) < text_counts[0]).astype(jnp.float32)
    text_emb = unit_rows(text_rows.astype(jnp.float32)).astype(jnp.bfloat16)
    logit_mul = logit_scale[0]
    logit_add = logit_bias[0]
    width = text_emb.shape[1]

    def terms_from(text_block, source):
        first_id = (source * width_shards + width_index) * rows_dev
        block_ids = lax.dynamic_slice_in_dim(text_ids, first_id, rows_dev, 0)
        return pair_terms(
            text_block, block_ids, image_emb, image_ids, image_valid, logit_mul, logit_add
        )

    def pass_text(text_block):
        return from_behind(text_block, "dp", 1)

    def pass_grad(totals):
        return from_behind(totals, "dp", 1)

    def visit_block(hop_index, carried):
        text_block, totals = carried
        source = (data_index - hop_index) % data_shards
        totals = totals + terms_from(text_block, source)
        return (pass_text(text_block), pass_grad(totals))

    start_state = (text_emb, jnp.zeros((rows_dev, width), jnp.float32))
    text_block, totals = lax.fori_loop(0, data_shards - 1, visit_block, start_state)
    totals = totals + terms_from(text_block, (data_index + 1) % data_shards)
    text_grad = pass_grad(totals)
    return text_grad * text_valid[:, None]


def solution(mesh):
    placed = (
        P("dp", None, None),
        P("dp", None),
        P("dp"),
        P(),
        P(),
        P(None, "mp"),
        P("mp", None),
        P(("dp", "mp"), None),
        P(("dp", "mp")),
        P(),
        P(),
        P(),
    )
    return jax.shard_map(
        local, mesh=mesh, in_specs=placed, out_specs=P(("dp", "mp"), None), check_vma=False
    )
```

profile of v0, /device:TPU:0, one launch (start us, length us, event | category | flops | bytes accessed | tf_op | source)
XLA Modules:
  0.0 76.1 jit_solution(1497484599802272056)
XLA Ops:
  0.0 0.0 copy-start
  0.0 1.9 %convert_reduce_fusion.1 = (f32[16,1152]{1,0:T(8,128)S(1)}, f32[16,32]{1,0:T(8,128)S(1)}) fusion(bf16[16,32,1152]{2,1,0:T(8,128)(2,1)} %param.16), kind=kLoop, calls=%fused_computation.27 | loop fusion | flops 1750528 | bytes 1255424 | tf_op jit(solution)/shard_map/reduce_sum | solution.py:65
  1.9 0.5 fusion.24
  2.4 3.1 %convert_reduce_fusion.2 = f32[16,768]{1,0:T(8,128)S(1)} fusion(bf16[1152,768]{1,0:T(8,128)(2,1)} %param.21, bf16[16,32,1152]{2,1,0:T(8,128)(2,1)S(1)} %copy-done.2, f32[1152]{0:T(1024)S(1)} %copy-done.5, f32[1152]{0:T(1024)S(1)} %copy-done.6, f32[16,32]{1,0:T(8,128)S(1)} %add_rsqrt_fusion, f32[16,32]{1,0:T(8,128)S(1)} %broadcast_multiply_fusion.1), kind=kOutput, calls=%fused_computation.47 | convolution fusion | flops 913821696 | bytes 3011584 | tf_op jit(solution)/shard_map/dot_general | solution.py:60
  5.5 0.0 copy-start.4
  5.5 0.0 copy-start.1
  5.5 0.0 copy-start.3
  5.5 0.0 copy-start.7
  5.5 0.0 copy-start.8
  5.5 0.3 convolution_convert_fusion
  5.9 21.2 %psum.7 = bf16[16,1152]{1,0:T(8,128)(2,1)S(1)} all-reduce(bf16[16,1152]{1,0:T(8,128)(2,1)S(1)} %convolution_convert_fusion), channel_id=1, replica_groups=mesh['dp'=8,'mp'=4] {'mp'}, use_global_device_ids=true, to_apply=%region_5.0 | all-reduce | flops 18432 | bytes 73728 | tf_op jit(solution)/shard_map/psum | solution.py:66
  27.1 0.1 multiply_reduce_fusion
  27.3 0.1 multiply_convert_fusion
  27.4 0.7 gather_fusion
  28.1 0.1 fusion.59
  28.2 0.1 fusion.60
  29.6 0.1 dynamic_slice.13
  29.7 41.3 %while.18 = (s32[]{:T(128)}, bf16[4,1152]{1,0:T(4,128)(2,1)S(1)}, f32[4,1152]{1,0:T(4,128)S(1)}, f32[16]{0:T(128)S(1)}, s32[]{:T(128)}, /*index=5*/s32[]{:T(128)...) while((s32[]{:T(128)}, bf16[4,1152]{1,0:T(4,128)(2,1)S(1)}, ...), condition=%wide.region_8.9_spmd, body=%wide.region_7.8_spmd.sunk | while | flops 300372 | bytes 212584 | solution.py:100
  29.7 0.1 dynamic_slice.15
  29.8 1.6 %convolution_add_fusion.3 = f32[4,1152]{1,0:T(4,128)S(1)} fusion(f32[4,1152]{1,0:T(4,128)S(1)} %get-tuple-element.395, bf16[16,1152]{1,0:T(8,128)(2,1)S(1)} %get-tuple-element.419, bf16[4,1152]{1,0:T(4,128)(2,1)S(1)} %copy.17, f32[]{:T(128)} %get-tuple-element.420, f32[]{:T(128)} %get-tuple-element.418, s32[16]{0:T(128)S(1)} %get-tuple-element.417, ...), kind=kOutput, calls=%fused_computation.1.clone.1 | convolution fusion | flops 300352 | bytes 83096 | tf_op jit(solution)/shard_map/while/body/eval_jaxpr/dot_general | solution.py:36
  31.3 0.1 collective-permute-start.1
  31.4 1.6 %collective-permute-start = (bf16[4,1152]{1,0:T(4,128)(2,1)S(1)}, bf16[4,1152]{1,0:T(4,128)(2,1)S(1)}, u32[]{:S(2)}, u32[]{:S(2)}) collective-permute-start(bf16[4,1152]{1,0:T(4,128)(2,1)S(1)} %copy.17), channel_id=1, source_target_pairs={{28,0},{0,4},{4,8},{8,12},{12,16},{16,20},{20,24},{24,28},{29,1},{... | collective-permute-start | bytes 27656 | tf_op jit(solution)/shard_map/while/body/eval_jaxpr/ppermute | solution.py:12
  33.0 2.6 %collective-permute-done = bf16[4,1152]{1,0:T(4,128)(2,1)S(1)} collective-permute-done((bf16[4,1152]{1,0:T(4,128)(2,1)S(1)}, bf16[4,1152]{1,0:T(4,128)(2,1)S(1)}, u32[]{:S(2)}, u32[]{:S(2)}) %collective-permute-start) | collective-permute-done | bytes 9248 | tf_op jit(solution)/shard_map/while/body/eval_jaxpr/ppermute | solution.py:12
  35.6 0.0 collective-permute-done.1
  35.6 0.1 dynamic_slice.15
  35.7 1.6 %convolution_add_fusion.3 = f32[4,1152]{1,0:T(4,128)S(1)} fusion(f32[4,1152]{1,0:T(4,128)S(1)} %get-tuple-element.395, bf16[16,1152]{1,0:T(8,128)(2,1)S(1)} %get-tuple-element.419, bf16[4,1152]{1,0:T(4,128)(2,1)S(1)} %copy.17, f32[]{:T(128)} %get-tuple-element.420, f32[]{:T(128)} %get-tuple-element.418, s32[16]{0:T(128)S(1)} %get-tuple-element.417, ...), kind=kOutput, calls=%fused_computation.1.clone.1 | convolution fusion | flops 300352 | bytes 83096 | tf_op jit(solution)/shard_map/while/body/eval_jaxpr/dot_general | solution.py:36
  37.2 0.1 collective-permute-start.1
  37.3 0.7 collective-permute-start
  38.0 3.5 %collective-permute-done = bf16[4,1152]{1,0:T(4,128)(2,1)S(1)} collective-permute-done((bf16[4,1152]{1,0:T(4,128)(2,1)S(1)}, bf16[4,1152]{1,0:T(4,128)(2,1)S(1)}, u32[]{:S(2)}, u32[]{:S(2)}) %collective-permute-start) | collective-permute-done | bytes 9248 | tf_op jit(solution)/shard_map/while/body/eval_jaxpr/ppermute | solution.py:12
  41.5 0.0 collective-permute-done.1
  41.5 0.1 dynamic_slice.15
  41.6 1.6 %convolution_add_fusion.3 = f32[4,1152]{1,0:T(4,128)S(1)} fusion(f32[4,1152]{1,0:T(4,128)S(1)} %get-tuple-element.395, bf16[16,1152]{1,0:T(8,128)(2,1)S(1)} %get-tuple-element.419, bf16[4,1152]{1,0:T(4,128)(2,1)S(1)} %copy.17, f32[]{:T(128)} %get-tuple-element.420, f32[]{:T(128)} %get-tuple-element.418, s32[16]{0:T(128)S(1)} %get-tuple-element.417, ...), kind=kOutput, calls=%fused_computation.1.clone.1 | convolution fusion | flops 300352 | bytes 83096 | tf_op jit(solution)/shard_map/while/body/eval_jaxpr/dot_general | solution.py:36
  43.1 0.1 collective-permute-start.1
  43.2 0.1 collective-permute-start
  43.3 4.1 %collective-permute-done = bf16[4,1152]{1,0:T(4,128)(2,1)S(1)} collective-permute-done((bf16[4,1152]{1,0:T(4,128)(2,1)S(1)}, bf16[4,1152]{1,0:T(4,128)(2,1)S(1)}, u32[]{:S(2)}, u32[]{:S(2)}) %collective-permute-start) | collective-permute-done | bytes 9248 | tf_op jit(solution)/shard_map/while/body/eval_jaxpr/ppermute | solution.py:12
  47.4 0.0 collective-permute-done.1
  47.4 0.1 dynamic_slice.15
  47.5 1.6 %convolution_add_fusion.3 = f32[4,1152]{1,0:T(4,128)S(1)} fusion(f32[4,1152]{1,0:T(4,128)S(1)} %get-tuple-element.395, bf16[16,1152]{1,0:T(8,128)(2,1)S(1)} %get-tuple-element.419, bf16[4,1152]{1,0:T(4,128)(2,1)S(1)} %copy.17, f32[]{:T(128)} %get-tuple-element.420, f32[]{:T(128)} %get-tuple-element.418, s32[16]{0:T(128)S(1)} %get-tuple-element.417, ...), kind=kOutput, calls=%fused_computation.1.clone.1 | convolution fusion | flops 300352 | bytes 83096 | tf_op jit(solution)/shard_map/while/body/eval_jaxpr/dot_general | solution.py:36
  49.0 0.1 collective-permute-start.1
  49.1 0.1 collective-permute-start
  49.2 4.1 %collective-permute-done = bf16[4,1152]{1,0:T(4,128)(2,1)S(1)} collective-permute-done((bf16[4,1152]{1,0:T(4,128)(2,1)S(1)}, bf16[4,1152]{1,0:T(4,128)(2,1)S(1)}, u32[]{:S(2)}, u32[]{:S(2)}) %collective-permute-start) | collective-permute-done | bytes 9248 | tf_op jit(solution)/shard_map/while/body/eval_jaxpr/ppermute | solution.py:12
  53.3 0.0 collective-permute-done.1
  53.3 0.1 dynamic_slice.15
  53.4 1.6 %convolution_add_fusion.3 = f32[4,1152]{1,0:T(4,128)S(1)} fusion(f32[4,1152]{1,0:T(4,128)S(1)} %get-tuple-element.395, bf16[16,1152]{1,0:T(8,128)(2,1)S(1)} %get-tuple-element.419, bf16[4,1152]{1,0:T(4,128)(2,1)S(1)} %copy.17, f32[]{:T(128)} %get-tuple-element.420, f32[]{:T(128)} %get-tuple-element.418, s32[16]{0:T(128)S(1)} %get-tuple-element.417, ...), kind=kOutput, calls=%fused_computation.1.clone.1 | convolution fusion | flops 300352 | bytes 83096 | tf_op jit(solution)/shard_map/while/body/eval_jaxpr/dot_general | solution.py:36
  54.9 0.1 collective-permute-start.1
  55.0 0.1 collective-permute-start
  55.1 4.1 %collective-permute-done = bf16[4,1152]{1,0:T(4,128)(2,1)S(1)} collective-permute-done((bf16[4,1152]{1,0:T(4,128)(2,1)S(1)}, bf16[4,1152]{1,0:T(4,128)(2,1)S(1)}, u32[]{:S(2)}, u32[]{:S(2)}) %collective-permute-start) | collective-permute-done | bytes 9248 | tf_op jit(solution)/shard_map/while/body/eval_jaxpr/ppermute | solution.py:12
  59.2 0.0 collective-permute-done.1
  59.2 0.1 dynamic_slice.15
  59.3 1.6 %convolution_add_fusion.3 = f32[4,1152]{1,0:T(4,128)S(1)} fusion(f32[4,1152]{1,0:T(4,128)S(1)} %get-tuple-element.395, bf16[16,1152]{1,0:T(8,128)(2,1)S(1)} %get-tuple-element.419, bf16[4,1152]{1,0:T(4,128)(2,1)S(1)} %copy.17, f32[]{:T(128)} %get-tuple-element.420, f32[]{:T(128)} %get-tuple-element.418, s32[16]{0:T(128)S(1)} %get-tuple-element.417, ...), kind=kOutput, calls=%fused_computation.1.clone.1 | convolution fusion | flops 300352 | bytes 83096 | tf_op jit(solution)/shard_map/while/body/eval_jaxpr/dot_general | solution.py:36
  60.8 0.1 collective-permute-start.1
  60.9 0.1 collective-permute-start
  61.0 4.1 %collective-permute-done = bf16[4,1152]{1,0:T(4,128)(2,1)S(1)} collective-permute-done((bf16[4,1152]{1,0:T(4,128)(2,1)S(1)}, bf16[4,1152]{1,0:T(4,128)(2,1)S(1)}, u32[]{:S(2)}, u32[]{:S(2)}) %collective-permute-start) | collective-permute-done | bytes 9248 | tf_op jit(solution)/shard_map/while/body/eval_jaxpr/ppermute | solution.py:12
  65.1 0.0 collective-permute-done.1
  65.1 0.1 dynamic_slice.15
  65.2 1.6 %convolution_add_fusion.3 = f32[4,1152]{1,0:T(4,128)S(1)} fusion(f32[4,1152]{1,0:T(4,128)S(1)} %get-tuple-element.395, bf16[16,1152]{1,0:T(8,128)(2,1)S(1)} %get-tuple-element.419, bf16[4,1152]{1,0:T(4,128)(2,1)S(1)} %copy.17, f32[]{:T(128)} %get-tuple-element.420, f32[]{:T(128)} %get-tuple-element.418, s32[16]{0:T(128)S(1)} %get-tuple-element.417, ...), kind=kOutput, calls=%fused_computation.1.clone.1 | convolution fusion | flops 300352 | bytes 83096 | tf_op jit(solution)/shard_map/while/body/eval_jaxpr/dot_general | solution.py:36
  66.7 0.1 collective-permute-start.1
  66.8 0.1 collective-permute-start
  66.9 4.1 %collective-permute-done = bf16[4,1152]{1,0:T(4,128)(2,1)S(1)} collective-permute-done((bf16[4,1152]{1,0:T(4,128)(2,1)S(1)}, bf16[4,1152]{1,0:T(4,128)(2,1)S(1)}, u32[]{:S(2)}, u32[]{:S(2)}) %collective-permute-start) | collective-permute-done | bytes 9248 | tf_op jit(solution)/shard_map/while/body/eval_jaxpr/ppermute | solution.py:12
  71.0 0.0 collective-permute-done.1
  71.0 0.3 convolution_add_fusion.1
  71.3 0.1 collective-permute-start.2
  72.0 3.4 %collective-permute-done.2 = f32[4,1152]{1,0:T(4,128)S(1)} collective-permute-done((f32[4,1152]{1,0:T(4,128)S(1)}, f32[4,1152]{1,0:T(4,128)S(1)}, u32[]{:S(2)}, u32[]{:S(2)}) %collective-permute-start.2) | collective-permute-done | bytes 18464 | tf_op jit(solution)/shard_map/ppermute | solution.py:12
  75.4 0.7 broadcast_multiply_fusion
  (27 shorter events, 0.1 us)
Async XLA Ops:
  0.0 5.5 %copy-start = (bf16[768,1152]{1,0:T(8,128)(2,1)S(1)}, bf16[768,1152]{1,0:T(8,128)(2,1)}, u32[]{:S(2)}) copy-start(bf16[768,1152]{1,0:T(8,128)(2,1)} %param.22) | copy-start | bytes 5308420
  0.0 1.9 %copy-start.2 = (bf16[16,32,1152]{2,1,0:T(8,128)(2,1)S(1)}, bf16[16,32,1152]{2,1,0:T(8,128)(2,1)}, u32[]{:S(2)}) copy-start(bf16[16,32,1152]{2,1,0:T(8,128)(2,1)} %param.16) | copy-start | bytes 3538948
  0.0 2.4 %copy-start.6 = (f32[1152]{0:T(1024)S(1)}, f32[1152]{0:T(1024)}, u32[]{:S(2)}) copy-start(f32[1152]{0:T(1024)} %param.19) | copy-start | bytes 13828
  0.0 2.4 %copy-start.5 = (f32[1152]{0:T(1024)S(1)}, f32[1152]{0:T(1024)}, u32[]{:S(2)}) copy-start(f32[1152]{0:T(1024)} %param.20) | copy-start | bytes 13828
  5.5 21.9 %copy-start.4 = (s32[16]{0:T(128)S(1)}, s32[16]{0:T(128)}, u32[]{:S(2)}) copy-start(s32[16]{0:T(128)} %constant.240) | copy-start | bytes 196
  5.5 21.9 %copy-start.1 = (s32[1,4]{1,0:T(1,128)S(1)}, s32[1,4]{1,0:T(1,128)}, u32[]{:S(2)}) copy-start(s32[1,4]{1,0:T(1,128)} %param.17) | copy-start | bytes 52
  5.5 22.5 %copy-start.3 = (bf16[4,1152]{1,0:T(4,128)(2,1)S(1)}, bf16[4,1152]{1,0:T(4,128)(2,1)}, u32[]{:S(2)}) copy-start(bf16[4,1152]{1,0:T(4,128)(2,1)} %param.23) | copy-start | bytes 27652
  5.5 24.1 %copy-start.7 = (s32[128]{0:T(128)S(1)}, s32[128]{0:T(128)}, u32[]{:S(2)}) copy-start(s32[128]{0:T(128)} %param.25) | copy-start | bytes 1540
  5.5 24.1 %copy-start.8 = (s32[16]{0:T(128)S(1)}, s32[16]{0:T(128)}, u32[]{:S(2)}) copy-start(s32[16]{0:T(128)} %param.18) | copy-start | bytes 196
  31.3 4.2 %collective-permute-start.1 = (f32[4,1152]{1,0:T(4,128)S(1)}, f32[4,1152]{1,0:T(4,128)S(1)}, u32[]{:S(2)}, u32[]{:S(2)}) collective-permute-start(f32[4,1152]{1,0:T(4,128)S(1)} %convolution_add_fusion.3), channel_id=1, source_target_pairs={{28,0},{0,4},{4,8},{8,12},{12,16},{16,20},{20,24},{24,28},{29,1},{... | collective-permute-start | bytes 55304 | tf_op jit(solution)/shard_map/while/body/eval_jaxpr/ppermute | solution.py:12
  31.4 4.2 %collective-permute-start = (bf16[4,1152]{1,0:T(4,128)(2,1)S(1)}, bf16[4,1152]{1,0:T(4,128)(2,1)S(1)}, u32[]{:S(2)}, u32[]{:S(2)}) collective-permute-start(bf16[4,1152]{1,0:T(4,128)(2,1)S(1)} %copy.17), channel_id=1, source_target_pairs={{28,0},{0,4},{4,8},{8,12},{12,16},{16,20},{20,24},{24,28},{29,1},{... | collective-permute-start | bytes 27656 | tf_op jit(solution)/shard_map/while/body/eval_jaxpr/ppermute | solution.py:12
  37.2 4.2 %collective-permute-start.1 = (f32[4,1152]{1,0:T(4,128)S(1)}, f32[4,1152]{1,0:T(4,128)S(1)}, u32[]{:S(2)}, u32[]{:S(2)}) collective-permute-start(f32[4,1152]{1,0:T(4,128)S(1)} %convolution_add_fusion.3), channel_id=1, source_target_pairs={{28,0},{0,4},{4,8},{8,12},{12,16},{16,20},{20,24},{24,28},{29,1},{... | collective-permute-start | bytes 55304 | tf_op jit(solution)/shard_map/while/body/eval_jaxpr/ppermute | solution.py:12
  37.3 4.2 %collective-permute-start = (bf16[4,1152]{1,0:T(4,128)(2,1)S(1)}, bf16[4,1152]{1,0:T(4,128)(2,1)S(1)}, u32[]{:S(2)}, u32[]{:S(2)}) collective-permute-start(bf16[4,1152]{1,0:T(4,128)(2,1)S(1)} %copy.17), channel_id=1, source_target_pairs={{28,0},{0,4},{4,8},{8,12},{12,16},{16,20},{20,24},{24,28},{29,1},{... | collective-permute-start | bytes 27656 | tf_op jit(solution)/shard_map/while/body/eval_jaxpr/ppermute | solution.py:12
  43.1 4.2 %collective-permute-start.1 = (f32[4,1152]{1,0:T(4,128)S(1)}, f32[4,1152]{1,0:T(4,128)S(1)}, u32[]{:S(2)}, u32[]{:S(2)}) collective-permute-start(f32[4,1152]{1,0:T(4,128)S(1)} %convolution_add_fusion.3), channel_id=1, source_target_pairs={{28,0},{0,4},{4,8},{8,12},{12,16},{16,20},{20,24},{24,28},{29,1},{... | collective-permute-start | bytes 55304 | tf_op jit(solution)/shard_map/while/body/eval_jaxpr/ppermute | solution.py:12
  43.2 4.2 %collective-permute-start = (bf16[4,1152]{1,0:T(4,128)(2,1)S(1)}, bf16[4,1152]{1,0:T(4,128)(2,1)S(1)}, u32[]{:S(2)}, u32[]{:S(2)}) collective-permute-start(bf16[4,1152]{1,0:T(4,128)(2,1)S(1)} %copy.17), channel_id=1, source_target_pairs={{28,0},{0,4},{4,8},{8,12},{12,16},{16,20},{20,24},{24,28},{29,1},{... | collective-permute-start | bytes 27656 | tf_op jit(solution)/shard_map/while/body/eval_jaxpr/ppermute | solution.py:12
  49.0 4.2 %collective-permute-start.1 = (f32[4,1152]{1,0:T(4,128)S(1)}, f32[4,1152]{1,0:T(4,128)S(1)}, u32[]{:S(2)}, u32[]{:S(2)}) collective-permute-start(f32[4,1152]{1,0:T(4,128)S(1)} %convolution_add_fusion.3), channel_id=1, source_target_pairs={{28,0},{0,4},{4,8},{8,12},{12,16},{16,20},{20,24},{24,28},{29,1},{... | collective-permute-start | bytes 55304 | tf_op jit(solution)/shard_map/while/body/eval_jaxpr/ppermute | solution.py:12
  49.1 4.2 %collective-permute-start = (bf16[4,1152]{1,0:T(4,128)(2,1)S(1)}, bf16[4,1152]{1,0:T(4,128)(2,1)S(1)}, u32[]{:S(2)}, u32[]{:S(2)}) collective-permute-start(bf16[4,1152]{1,0:T(4,128)(2,1)S(1)} %copy.17), channel_id=1, source_target_pairs={{28,0},{0,4},{4,8},{8,12},{12,16},{16,20},{20,24},{24,28},{29,1},{... | collective-permute-start | bytes 27656 | tf_op jit(solution)/shard_map/while/body/eval_jaxpr/ppermute | solution.py:12
  54.9 4.2 %collective-permute-start.1 = (f32[4,1152]{1,0:T(4,128)S(1)}, f32[4,1152]{1,0:T(4,128)S(1)}, u32[]{:S(2)}, u32[]{:S(2)}) collective-permute-start(f32[4,1152]{1,0:T(4,128)S(1)} %convolution_add_fusion.3), channel_id=1, source_target_pairs={{28,0},{0,4},{4,8},{8,12},{12,16},{16,20},{20,24},{24,28},{29,1},{... | collective-permute-start | bytes 55304 | tf_op jit(solution)/shard_map/while/body/eval_jaxpr/ppermute | solution.py:12
  55.0 4.2 %collective-permute-start = (bf16[4,1152]{1,0:T(4,128)(2,1)S(1)}, bf16[4,1152]{1,0:T(4,128)(2,1)S(1)}, u32[]{:S(2)}, u32[]{:S(2)}) collective-permute-start(bf16[4,1152]{1,0:T(4,128)(2,1)S(1)} %copy.17), channel_id=1, source_target_pairs={{28,0},{0,4},{4,8},{8,12},{12,16},{16,20},{20,24},{24,28},{29,1},{... | collective-permute-start | bytes 27656 | tf_op jit(solution)/shard_map/while/body/eval_jaxpr/ppermute | solution.py:12
  60.8 4.2 %collective-permute-start.1 = (f32[4,1152]{1,0:T(4,128)S(1)}, f32[4,1152]{1,0:T(4,128)S(1)}, u32[]{:S(2)}, u32[]{:S(2)}) collective-permute-start(f32[4,1152]{1,0:T(4,128)S(1)} %convolution_add_fusion.3), channel_id=1, source_target_pairs={{28,0},{0,4},{4,8},{8,12},{12,16},{16,20},{20,24},{24,28},{29,1},{... | collective-permute-start | bytes 55304 | tf_op jit(solution)/shard_map/while/body/eval_jaxpr/ppermute | solution.py:12
  60.9 4.2 %collective-permute-start = (bf16[4,1152]{1,0:T(4,128)(2,1)S(1)}, bf16[4,1152]{1,0:T(4,128)(2,1)S(1)}, u32[]{:S(2)}, u32[]{:S(2)}) collective-permute-start(bf16[4,1152]{1,0:T(4,128)(2,1)S(1)} %copy.17), channel_id=1, source_target_pairs={{28,0},{0,4},{4,8},{8,12},{12,16},{16,20},{20,24},{24,28},{29,1},{... | collective-permute-start | bytes 27656 | tf_op jit(solution)/shard_map/while/body/eval_jaxpr/ppermute | solution.py:12
  66.7 4.2 %collective-permute-start.1 = (f32[4,1152]{1,0:T(4,128)S(1)}, f32[4,1152]{1,0:T(4,128)S(1)}, u32[]{:S(2)}, u32[]{:S(2)}) collective-permute-start(f32[4,1152]{1,0:T(4,128)S(1)} %convolution_add_fusion.3), channel_id=1, source_target_pairs={{28,0},{0,4},{4,8},{8,12},{12,16},{16,20},{20,24},{24,28},{29,1},{... | collective-permute-start | bytes 55304 | tf_op jit(solution)/shard_map/while/body/eval_jaxpr/ppermute | solution.py:12
  66.8 4.2 %collective-permute-start = (bf16[4,1152]{1,0:T(4,128)(2,1)S(1)}, bf16[4,1152]{1,0:T(4,128)(2,1)S(1)}, u32[]{:S(2)}, u32[]{:S(2)}) collective-permute-start(bf16[4,1152]{1,0:T(4,128)(2,1)S(1)} %copy.17), channel_id=1, source_target_pairs={{28,0},{0,4},{4,8},{8,12},{12,16},{16,20},{20,24},{24,28},{29,1},{... | collective-permute-start | bytes 27656 | tf_op jit(solution)/shard_map/while/body/eval_jaxpr/ppermute | solution.py:12
  71.3 4.1 %collective-permute-start.2 = (f32[4,1152]{1,0:T(4,128)S(1)}, f32[4,1152]{1,0:T(4,128)S(1)}, u32[]{:S(2)}, u32[]{:S(2)}) collective-permute-start(f32[4,1152]{1,0:T(4,128)S(1)} %convolution_add_fusion.1), channel_id=1, source_target_pairs={{28,0},{0,4},{4,8},{8,12},{12,16},{16,20},{20,24},{24,28},{29,1},{... | collective-permute-start | bytes 55304 | tf_op jit(solution)/shard_map/ppermute | solution.py:12
where the time goes:
time: 76.4 us; the launch traced here: 76.1 us
  waiting for transfers between devices  30 us (39%)
  blocking collectives  21.2 us (28%)
  matrix products  14.6 us (19%)
  other arithmetic  3.44 us (5%)
  starting transfers between devices  3.01 us (4%)
  between operations  2.13 us (3%)
  local copies, waits for them, and re-layouts  1.37 us (2%)
    ppermute x15, waiting for transfers between devices, from_behind(): return lax.ppermute(block, axis, route)  30 us
    psum x1, blocking collectives, local(): lax.psum(partial_value.astype(jnp.bfloat16), 'mp').astype(jnp.float32)  21.2 us
    dot_general x8, matrix products, pair_terms(): return jnp.dot(weights, image_emb, preferred_element_type=jnp.float32)  11.2 us
    dot_general x1, matrix products, local(): jnp.dot(normed, up_weight, preferred_element_type=jnp.float32)  3.09 us
    ppermute x15, starting transfers between devices, from_behind(): return lax.ppermute(block, axis, route)  3.01 us
    reduce_sum x1, other arithmetic, local(): pooled_tokens = jnp.mean(image_tokens.astype(jnp.float32), axis=1)  1.85 us
  transfers between devices with their start and end apart: 15, of which 8 were waited for; matrix products, arithmetic and copies ran while one was open for 0% of the time, Pallas kernels for 0%

commit v1 on v0

v1 whole, which is shorter than its diff:
```python
import functools

import jax
import jax.numpy as jnp
from jax import lax
from jax.experimental import pallas as pl
from jax.experimental.pallas import tpu as pltpu
from jax.sharding import PartitionSpec as P

norm_eps = 1e-06


def unit_rows(values):
    return values * lax.rsqrt(jnp.sum(values * values, axis=-1, keepdims=True) + norm_eps)


def gelu(x):
    inner = x * (0.7978845608028654 + (0.7978845608028654 * 0.044715) * (x * x))
    return 0.5 * x * (1.0 + jnp.tanh(inner))


def kernel(
    dp,
    mp,
    chunk,
    tokens_hbm,
    image_counts,
    image_ids,
    gain,
    shift,
    up_hbm,
    down_hbm,
    text_rows,
    text_counts,
    text_ids,
    logit_scale,
    logit_bias,
    out,
    tokens,
    up,
    down,
    pooled_tokens,
    pooled_hidden,
    text_all,
    part_send,
    part_recv,
    grad_send,
    grad_recv,
    token_sem,
    up_sem,
    down_sem,
    text_ssem,
    text_rsem,
    part_ssem,
    part_rsem,
    grad_ssem,
    grad_rsem,
):
    images, patches, width = tokens.shape
    rows_dev = text_rows.shape[0]
    chunks = images // chunk
    texts = dp * rows_dev
    my_d = lax.axis_index("dp")
    my_m = lax.axis_index("mp")

    def token_copy(c):
        part = pl.ds(c * chunk, chunk)
        return pltpu.make_async_copy(tokens_hbm.at[part], tokens.at[part], token_sem.at[c])

    def behind(axis, size, me, o):
        return {axis: lax.rem(me + (size - o), size)}

    def ahead(axis, size, me, o):
        return {axis: lax.rem(me + o, size)}

    up_copy = pltpu.make_async_copy(up_hbm, up, up_sem)
    down_copy = pltpu.make_async_copy(down_hbm, down, down_sem)
    token_copy(0).start()
    up_copy.start()
    for c in range(1, chunks):
        token_copy(c).start()
    down_copy.start()

    barrier = pltpu.get_barrier_semaphore()
    for o in range(1, mp):
        pl.semaphore_signal(barrier, inc=1, device_id=ahead("mp", mp, my_m, o))
    for o in range(1, dp):
        pl.semaphore_signal(barrier, inc=1, device_id=ahead("dp", dp, my_d, o))

    def visit(c):
        token_copy(c).wait()
        first = pl.multiple_of(c * chunk, chunk)
        block = tokens[pl.ds(first, chunk)].astype(jnp.float32)
        pooled_tokens[pl.ds(first, chunk), :] = jnp.sum(block, axis=1) * (1.0 / patches)
        values = block.reshape(chunk * patches, width)
        center = jnp.mean(values, axis=-1, keepdims=True)
        values = values - center
        spread = jnp.mean(values * values, axis=-1, keepdims=True)
        normed = values * lax.rsqrt(spread + norm_eps) * gain[...].reshape(1, -1) + shift[...].reshape(1, -1)
        normed = normed.astype(jnp.bfloat16)
        return first, normed

    def finish(first, normed):
        hidden = gelu(jnp.dot(normed, up[...], preferred_element_type=jnp.float32))
        hidden = hidden.reshape(chunk, patches, hidden.shape[-1])
        pooled_hidden[pl.ds(first, chunk), :] = jnp.sum(hidden, axis=1) * (1.0 / patches)

    def text_copy(o):
        return pltpu.make_async_remote_copy(
            src_ref=text_rows,
            dst_ref=text_all.at[o - 1],
            send_sem=text_ssem.at[o - 1],
            recv_sem=text_rsem.at[o - 1],
            device_id=ahead("dp", dp, my_d, o),
        )

    def part_copy(o):
        return pltpu.make_async_remote_copy(
            src_ref=part_send,
            dst_ref=part_recv.at[o - 1],
            send_sem=part_ssem.at[o - 1],
            recv_sem=part_rsem.at[o - 1],
            device_id=ahead("mp", mp, my_m, o),
        )

    def grad_copy(o):
        return pltpu.make_async_remote_copy(
            src_ref=grad_send.at[o - 1],
            dst_ref=grad_recv.at[o - 1],
            send_sem=grad_ssem.at[o - 1],
            recv_sem=grad_rsem.at[o - 1],
            device_id=behind("dp", dp, my_d, o),
        )

    first, normed = visit(0)
    up_copy.wait()
    finish(first, normed)
    pl.semaphore_wait(barrier, dp + mp - 2)
    for o in range(1, dp):
        text_copy(o).start()
    if chunks <= 4:
        for c in range(1, chunks):
            finish(*visit(c))
    else:

        @pl.loop(1, chunks)
        def _(c):
            finish(*visit(c))

    down_copy.wait()
    part = jnp.dot(
        pooled_hidden[...].astype(jnp.bfloat16), down[...], preferred_element_type=jnp.float32
    )
    part_send[...] = part.astype(jnp.bfloat16)
    for o in range(1, mp):
        part_copy(o).start()
    tower = part + pooled_tokens[...]

    row = lax.broadcasted_iota(jnp.int32, (texts, 1), 0)
    hop = row // rows_dev
    source = my_d - hop
    source = jnp.where(source < 0, source + dp, source)
    place = (source * mp + my_m) * rows_dev + (row - hop * rows_dev)
    id_count = text_ids.shape[1]
    column = lax.broadcasted_iota(jnp.int32, (texts, id_count), 1)
    block_ids = jnp.sum(
        jnp.where(column == place, text_ids[...], 0), axis=1, keepdims=True
    )
    slot = lax.broadcasted_iota(jnp.int32, (1, images), 1)
    group = slot // rows_dev
    counts = jnp.zeros((1, images), jnp.int32)
    for k in range(image_counts.shape[1]):
        counts = jnp.where(group == k, image_counts[:, k : k + 1], counts)
    scale = logit_scale[...].reshape(1, 1)
    sign = jnp.where(block_ids == image_ids[...], 1.0, -1.0).astype(jnp.float32)
    image_valid = (slot - group * rows_dev < counts).astype(jnp.float32)
    factor = image_valid * -sign * scale

    for o in range(1, dp):
        text_copy(o).wait_recv()
    text_emb = jnp.concatenate(
        [unit_rows(text_rows[...].astype(jnp.float32))]
        + [unit_rows(text_all[o - 1].astype(jnp.float32)) for o in range(1, dp)],
        axis=0,
    ).astype(jnp.bfloat16)

    for o in range(1, mp):
        part_copy(o).wait_recv()
        tower = tower + part_recv[o - 1].astype(jnp.float32)
    image_emb = unit_rows(tower).astype(jnp.bfloat16)
    cosines = lax.dot_general(
        text_emb, image_emb, (((1,), (1,)), ((), ())), preferred_element_type=jnp.float32
    )
    logits = scale * cosines + logit_bias[...].reshape(1, 1)
    weights = (factor * jax.nn.sigmoid(-sign * logits)).astype(jnp.bfloat16)
    grads = jnp.dot(weights, image_emb, preferred_element_type=jnp.float32)
    for o in range(1, dp):
        grad_send[o - 1] = grads[o * rows_dev : (o + 1) * rows_dev].astype(jnp.bfloat16)
        grad_copy(o).start()
    total = grads[:rows_dev]
    slots = lax.broadcasted_iota(jnp.int32, (rows_dev, 1), 0)
    text_valid = (slots < text_counts[...].reshape(1, 1)).astype(jnp.float32)
    for o in range(1, dp):
        grad_copy(o).wait_recv()
        total = total + grad_recv[o - 1].astype(jnp.float32)
    out[...] = total * text_valid
    for o in range(1, dp):
        text_copy(o).wait_send()
        grad_copy(o).wait_send()
    for o in range(1, mp):
        part_copy(o).wait_send()


def local(
    image_tokens,
    image_counts,
    image_ids,
    norm_gain,
    norm_bias,
    up_weight,
    down_weight,
    text_rows,
    text_counts,
    text_ids,
    logit_scale,
    logit_bias,
):
    dp = lax.axis_size("dp")
    mp = lax.axis_size("mp")
    images, patches, width = image_tokens.shape
    rows_dev = text_rows.shape[0]
    hidden = up_weight.shape[1]
    chunk = 8
    bf16, f32 = jnp.bfloat16, jnp.float32
    dma = pltpu.SemaphoreType.DMA
    vmem = pl.BlockSpec(memory_space=pltpu.VMEM)
    hbm = pl.BlockSpec(memory_space=pl.ANY)
    return pl.pallas_call(
        functools.partial(kernel, dp, mp, chunk),
        out_shape=jax.ShapeDtypeStruct((rows_dev, width), f32),
        in_specs=[hbm, vmem, vmem, vmem, vmem, hbm, hbm, vmem, vmem, vmem, vmem, vmem],
        out_specs=vmem,
        scratch_shapes=[
            pltpu.VMEM(image_tokens.shape, bf16),
            pltpu.VMEM(up_weight.shape, bf16),
            pltpu.VMEM(down_weight.shape, bf16),
            pltpu.VMEM((images, width), f32),
            pltpu.VMEM((images, hidden), f32),
            pltpu.VMEM((dp - 1, rows_dev, width), bf16),
            pltpu.VMEM((images, width), bf16),
            pltpu.VMEM((mp - 1, images, width), bf16),
            pltpu.VMEM((dp - 1, rows_dev, width), bf16),
            pltpu.VMEM((dp - 1, rows_dev, width), bf16),
            dma((images // chunk,)),
            dma,
            dma,
            dma((dp - 1,)),
            dma((dp - 1,)),
            dma((mp - 1,)),
            dma((mp - 1,)),
            dma((dp - 1,)),
            dma((dp - 1,)),
        ],
        compiler_params=pltpu.CompilerParams(collective_id=0, has_side_effects=True),
        name="tower_pair_grad",
    )(
        image_tokens,
        image_counts,
        image_ids.reshape(1, -1),
        norm_gain,
        norm_bias,
        up_weight,
        down_weight,
        text_rows,
        text_counts,
        text_ids.reshape(1, -1),
        logit_scale,
        logit_bias,
    )


def solution(mesh):
    placed = (
        P("dp", None, None),
        P("dp", None),
        P("dp"),
        P(),
        P(),
        P(None, "mp"),
        P("mp", None),
        P(("dp", "mp"), None),
        P(("dp", "mp")),
        P(),
        P(),
        P(),
    )
    return jax.shard_map(
        local, mesh=mesh, in_specs=placed, out_specs=P(("dp", "mp"), None), check_vma=False
    )
```

time: 76.4 us -> 21.8 us (0.29)
  waiting for transfers between devices: 30 us -> 0 us
  blocking collectives: 21.2 us -> 0 us
  Pallas kernels: 0 us -> 18.3 us
  matrix products: 14.6 us -> 0 us
  other arithmetic: 3.44 us -> 0 us
  starting transfers between devices: 3.01 us -> 0 us
    ppermute x15 -> x0, waiting for transfers between devices: 30 us -> none  [from_behind(): return lax.ppermute(block, axis, route)]
    psum x1 -> x0, blocking collectives: 21.2 us -> none  [local(): lax.psum(partial_value.astype(jnp.bfloat16), 'mp').astype(jnp.float32)]
    pallas_call x0 -> x1, Pallas kernels: none -> 18.3 us  [local(): pl.pallas_call(functools.partial(kernel, dp, mp, chunk), out_shape=jax.Sh...]
    dot_general x10 -> x0, matrix products: 14.6 us -> none  [the longest x8 11.2 us: pair_terms(): return jnp.dot(weights, image_emb, preferred_element_type=jnp.float32)]
    ppermute x15 -> x0, starting transfers between devices: 3.01 us -> none  [from_behind(): return lax.ppermute(block, axis, route)]
    reduce_sum x4 -> x0, other arithmetic: 2.56 us -> none  [the longest x1 1.85 us: local(): pooled_tokens = jnp.mean(image_tokens.astype(jnp.float32), axis=1)]
    unnamed x18 -> x1, local copies, waits for them, and re-layouts: 0.05 us -> 1.33 us
  transfers between devices with their start and end apart: 15 -> 0, of which waited for: 8 -> 0; matrix products, arithmetic and copies ran while one was open for 0% -> 0% of each run, Pallas kernels for 0% -> 0%
where the time goes in v1:
time: 21.8 us; the launch traced here: 21.5 us
  Pallas kernels  18.3 us (84%)
  between operations  1.95 us (9%)
  local copies, waits for them, and re-layouts  1.33 us (6%)
    pallas_call x1, Pallas kernels, local(): pl.pallas_call(functools.partial(kernel, dp, mp, chunk), out_shape=jax.Sh...  18.3 us
    unnamed x1, local copies, waits for them, and re-layouts  1.33 us

profile of v1, /device:TPU:0, one launch (start us, length us, event | category | flops | bytes accessed | tf_op | source)
XLA Modules:
  0.0 21.5 jit_solution(10497692712191189734)
XLA Ops:
  1.9 18.3 %tower_pair_grad.1 = f32[4,1152]{1,0:T(4,128)} custom-call(bf16[16,32,1152]{2,1,0:T(8,128)(2,1)} %tokens_hbm.1, s32[1,4]{1,0:T(1,128)} %image_counts.1, s32[1,16]{1,0:T(1,128)} %bitcast.2, f32[1152]{0:T(1024)} %gain.1, f32[1152]{0:T(1024)} %shift.1, bf16[1152,768]{1,0:T(8,128)(2,1)} %up_hbm.1, bf16[768,1152]{1,0:T(8,128)(2,1)} %down_hbm.1, ...), custom_call_target="tpu_custom_call" | custom-call | tf_op jit(solution)/shard_map/tower_pair_grad/pallas_call | solution.py:238
  20.2 1.3 %copy.17 = f32[4,1152]{1,0:T(4,128)} copy(f32[4,1152]{1,0:T(4,128)} %tower_pair_grad.1) | data formatting | bytes 36864

commit v2 on v1

v2 whole, which is shorter than its diff:
```python
import functools

import jax
import jax.numpy as jnp
from jax import lax
from jax.experimental import pallas as pl
from jax.experimental.pallas import tpu as pltpu
from jax.sharding import PartitionSpec as P

norm_eps = 1e-06


def unit_rows(values):
    return values * lax.rsqrt(jnp.sum(values * values, axis=-1, keepdims=True) + norm_eps)


def gelu(x):
    inner = x * (0.7978845608028654 + (0.7978845608028654 * 0.044715) * (x * x))
    return 0.5 * x * (1.0 + jnp.tanh(inner))


def kernel(
    dp,
    mp,
    chunk,
    tokens_hbm,
    counts_hbm,
    image_ids_hbm,
    gain_hbm,
    shift_hbm,
    up_hbm,
    down_hbm,
    text_hbm,
    text_counts_hbm,
    text_ids_hbm,
    scale_hbm,
    bias_hbm,
    out,
    tokens,
    up,
    down,
    image_counts,
    image_ids,
    gain,
    shift,
    text_rows,
    text_counts,
    text_ids,
    logit_scale,
    logit_bias,
    tower,
    pooled_hidden,
    text_all,
    part_send,
    part_recv,
    grad_send,
    grad_recv,
    token_sem,
    up_sem,
    down_sem,
    small_sem,
    text_ssem,
    text_rsem,
    part_ssem,
    part_rsem,
    grad_ssem,
    grad_rsem,
):
    images, patches, width = tokens.shape
    rows_dev = text_rows.shape[0]
    chunks = images // chunk
    texts = dp * rows_dev
    my_d = lax.axis_index("dp")
    my_m = lax.axis_index("mp")

    def token_copy(c):
        part = pl.ds(c * chunk, chunk)
        return pltpu.make_async_copy(tokens_hbm.at[part], tokens.at[part], token_sem.at[c])

    def behind(axis, size, me, o):
        return {axis: lax.rem(me + (size - o), size)}

    def ahead(axis, size, me, o):
        return {axis: lax.rem(me + o, size)}

    up_copy = pltpu.make_async_copy(up_hbm, up, up_sem)
    down_copy = pltpu.make_async_copy(down_hbm, down, down_sem)
    gain_copy = pltpu.make_async_copy(gain_hbm, gain, small_sem.at[0])
    shift_copy = pltpu.make_async_copy(shift_hbm, shift, small_sem.at[1])
    late = (
        (text_hbm, text_rows),
        (text_ids_hbm, text_ids),
        (image_ids_hbm, image_ids),
        (counts_hbm, image_counts),
        (text_counts_hbm, text_counts),
        (scale_hbm, logit_scale),
        (bias_hbm, logit_bias),
    )
    late_copies = [
        pltpu.make_async_copy(source, target, small_sem.at[2 + k])
        for k, (source, target) in enumerate(late)
    ]
    token_copy(0).start()
    gain_copy.start()
    shift_copy.start()
    up_copy.start()
    barrier = pltpu.get_barrier_semaphore()
    for o in range(1, mp):
        pl.semaphore_signal(barrier, inc=1, device_id=ahead("mp", mp, my_m, o))
    for o in range(1, dp):
        pl.semaphore_signal(barrier, inc=1, device_id=ahead("dp", dp, my_d, o))
    for c in range(1, chunks):
        token_copy(c).start()
    down_copy.start()
    for copy in late_copies:
        copy.start()

    pool_row = lax.broadcasted_iota(jnp.int32, (chunk, chunk * patches), 0)
    pool_column = lax.broadcasted_iota(jnp.int32, (chunk, chunk * patches), 1) // patches
    pool = jnp.where(pool_row == pool_column, 1.0 / patches, 0.0).astype(jnp.bfloat16)

    def visit(c):
        first = pl.multiple_of(c * chunk, chunk)
        block = tokens[pl.ds(first, chunk)].reshape(chunk * patches, width)
        tower[pl.ds(first, chunk), :] = jnp.dot(pool, block, preferred_element_type=jnp.float32)
        values = block.astype(jnp.float32)
        center = jnp.mean(values, axis=-1, keepdims=True)
        values = values - center
        spread = jnp.mean(values * values, axis=-1, keepdims=True)
        normed = (
            values * lax.rsqrt(spread + norm_eps) * gain[...].reshape(1, -1)
            + shift[...].reshape(1, -1)
        )
        return normed.astype(jnp.bfloat16)

    def finish(c, normed):
        first = pl.multiple_of(c * chunk, chunk)
        hidden = jnp.dot(normed, up[...], preferred_element_type=jnp.float32)
        hidden = gelu(hidden).astype(jnp.bfloat16)
        pooled_hidden[pl.ds(first, chunk), :] = jnp.dot(
            pool, hidden, preferred_element_type=jnp.float32
        )

    def text_copy(o):
        return pltpu.make_async_remote_copy(
            src_ref=text_hbm,
            dst_ref=text_all.at[o - 1],
            send_sem=text_ssem.at[o - 1],
            recv_sem=text_rsem.at[o - 1],
            device_id=ahead("dp", dp, my_d, o),
        )

    def part_copy(o, c):
        return pltpu.make_async_remote_copy(
            src_ref=part_send.at[c],
            dst_ref=part_recv.at[o - 1, c],
            send_sem=part_ssem.at[o - 1, c],
            recv_sem=part_rsem.at[o - 1, c],
            device_id=ahead("mp", mp, my_m, o),
        )

    def grad_copy(o):
        return pltpu.make_async_remote_copy(
            src_ref=grad_send.at[o - 1],
            dst_ref=grad_recv.at[o - 1],
            send_sem=grad_ssem.at[o - 1],
            recv_sem=grad_rsem.at[o - 1],
            device_id=behind("dp", dp, my_d, o),
        )

    def project(c):
        first = pl.multiple_of(c * chunk, chunk)
        pooled = pooled_hidden[pl.ds(first, chunk), :].astype(jnp.bfloat16)
        part = jnp.dot(pooled, down[...], preferred_element_type=jnp.float32)
        part_send[c] = part.astype(jnp.bfloat16)
        for o in range(1, mp):
            part_copy(o, c).start()
        tower[pl.ds(first, chunk), :] += part

    gain_copy.wait()
    shift_copy.wait()
    token_copy(0).wait()
    normed = visit(0)
    up_copy.wait()
    finish(0, normed)
    pl.semaphore_wait(barrier, dp + mp - 2)
    for o in range(1, dp):
        text_copy(o).start()
    if chunks <= 4:
        for c in range(1, chunks):
            token_copy(c).wait()
            normed = visit(c)
            if c == 1:
                down_copy.wait()
            project(c - 1)
            finish(c, normed)
        if chunks == 1:
            down_copy.wait()
    else:
        down_copy.wait()

        @pl.loop(1, chunks)
        def _(c):
            token_copy(c).wait()
            project(c - 1)
            finish(c, visit(c))

    project(chunks - 1)

    for copy in late_copies:
        copy.wait()
    row = lax.broadcasted_iota(jnp.int32, (texts, 1), 0)
    hop = row // rows_dev
    source = my_d - hop
    source = jnp.where(source < 0, source + dp, source)
    place = (source * mp + my_m) * rows_dev + (row - hop * rows_dev)
    id_count = text_ids.shape[1]
    column = lax.broadcasted_iota(jnp.int32, (texts, id_count), 1)
    block_ids = jnp.sum(jnp.where(column == place, text_ids[...], 0), axis=1, keepdims=True)
    slot = lax.broadcasted_iota(jnp.int32, (1, images), 1)
    group = slot // rows_dev
    counts = jnp.zeros((1, images), jnp.int32)
    for k in range(image_counts.shape[1]):
        counts = jnp.where(group == k, image_counts[:, k : k + 1], counts)
    scale = logit_scale[0]
    sign = jnp.where(block_ids == image_ids[...], 1.0, -1.0).astype(jnp.float32)
    image_valid = (slot - group * rows_dev < counts).astype(jnp.float32)
    factor = image_valid * -sign * scale

    for o in range(1, dp):
        text_copy(o).wait_recv()
    text_emb = jnp.concatenate(
        [unit_rows(text_rows[...].astype(jnp.float32))]
        + [unit_rows(text_all[o - 1].astype(jnp.float32)) for o in range(1, dp)],
        axis=0,
    ).astype(jnp.bfloat16)

    total = tower[...]
    for o in range(1, mp):
        for c in range(chunks):
            part_copy(o, c).wait_recv()
        total = total + part_recv[o - 1].astype(jnp.float32).reshape(images, width)
    image_emb = unit_rows(total).astype(jnp.bfloat16)
    cosines = lax.dot_general(
        text_emb, image_emb, (((1,), (1,)), ((), ())), preferred_element_type=jnp.float32
    )
    logits = scale * cosines + logit_bias[0]
    weights = (factor * jax.nn.sigmoid(-sign * logits)).astype(jnp.bfloat16)
    grads = jnp.dot(weights, image_emb, preferred_element_type=jnp.float32)
    for o in range(dp - 1, 0, -1):
        grad_send[o - 1] = grads[o * rows_dev : (o + 1) * rows_dev].astype(jnp.bfloat16)
        grad_copy(o).start()
    grad = grads[:rows_dev]
    slots = lax.broadcasted_iota(jnp.int32, (rows_dev, 1), 0)
    text_valid = (slots < text_counts[0]).astype(jnp.float32)
    for o in range(1, dp):
        grad_copy(o).wait_recv()
        grad = grad + grad_recv[o - 1].astype(jnp.float32)
    out[...] = grad * text_valid
    for o in range(1, dp):
        text_copy(o).wait_send()
        grad_copy(o).wait_send()
    for o in range(1, mp):
        for c in range(chunks):
            part_copy(o, c).wait_send()


def local(
    image_tokens,
    image_counts,
    image_ids,
    norm_gain,
    norm_bias,
    up_weight,
    down_weight,
    text_rows,
    text_counts,
    text_ids,
    logit_scale,
    logit_bias,
):
    dp = lax.axis_size("dp")
    mp = lax.axis_size("mp")
    images, patches, width = image_tokens.shape
    rows_dev = text_rows.shape[0]
    hidden = up_weight.shape[1]
    chunk = 8
    bf16, f32, i32 = jnp.bfloat16, jnp.float32, jnp.int32
    dma = pltpu.SemaphoreType.DMA
    vmem = pl.BlockSpec(memory_space=pltpu.VMEM)
    hbm = pl.BlockSpec(memory_space=pltpu.HBM)
    return pl.pallas_call(
        functools.partial(kernel, dp, mp, chunk),
        out_shape=pltpu.VMEM((rows_dev, width), f32),
        in_specs=[hbm] * 12,
        out_specs=vmem,
        scratch_shapes=[
            pltpu.VMEM(image_tokens.shape, bf16),
            pltpu.VMEM(up_weight.shape, bf16),
            pltpu.VMEM(down_weight.shape, bf16),
            pltpu.VMEM(image_counts.shape, i32),
            pltpu.VMEM((1, images), i32),
            pltpu.VMEM((width,), f32),
            pltpu.VMEM((width,), f32),
            pltpu.VMEM(text_rows.shape, bf16),
            pltpu.SMEM((1,), i32),
            pltpu.VMEM((1, text_ids.shape[0]), i32),
            pltpu.SMEM((1,), f32),
            pltpu.SMEM((1,), f32),
            pltpu.VMEM((images, width), f32),
            pltpu.VMEM((images, hidden), f32),
            pltpu.VMEM((dp - 1, rows_dev, width), bf16),
            pltpu.VMEM((images // chunk, chunk, width), bf16),
            pltpu.VMEM((mp - 1, images // chunk, chunk, width), bf16),
            pltpu.VMEM((dp - 1, rows_dev, width), bf16),
            pltpu.VMEM((dp - 1, rows_dev, width), bf16),
            dma((images // chunk,)),
            dma,
            dma,
            dma((9,)),
            dma((dp - 1,)),
            dma((dp - 1,)),
            dma((mp - 1, images // chunk)),
            dma((mp - 1, images // chunk)),
            dma((dp - 1,)),
            dma((dp - 1,)),
        ],
        compiler_params=pltpu.CompilerParams(collective_id=0, has_side_effects=True),
        name="tower_pair_grad",
    )(
        image_tokens,
        image_counts,
        image_ids.reshape(1, -1),
        norm_gain,
        norm_bias,
        up_weight,
        down_weight,
        text_rows,
        text_counts,
        text_ids.reshape(1, -1),
        logit_scale,
        logit_bias,
    )


def solution(mesh):
    placed = (
        P("dp", None, None),
        P("dp", None),
        P("dp"),
        P(),
        P(),
        P(None, "mp"),
        P("mp", None),
        P(("dp", "mp"), None),
        P(("dp", "mp")),
        P(),
        P(),
        P(),
    )
    return jax.shard_map(
        local, mesh=mesh, in_specs=placed, out_specs=P(("dp", "mp"), None), check_vma=False
    )
```

time: 21.8 us -> 19.4 us (0.89)
  Pallas kernels: 18.3 us -> 16.7 us
  local copies, waits for them, and re-layouts: 1.33 us -> 0.61 us
    pallas_call x1, Pallas kernels: 18.3 us -> 16.7 us  [local(): pl.pallas_call(functools.partial(kernel, dp, mp, chunk), out_shape=pltpu....]
    unnamed x1, local copies, waits for them, and re-layouts: 1.33 us -> 0.61 us
where the time goes in v2:
time: 19.4 us; the launch traced here: 19.2 us
  Pallas kernels  16.7 us (86%)
  between operations  1.95 us (10%)
  local copies, waits for them, and re-layouts  0.61 us (3%)
    pallas_call x1, Pallas kernels, local(): pl.pallas_call(functools.partial(kernel, dp, mp, chunk), out_shape=pltpu....  16.7 us
    unnamed x1, local copies, waits for them, and re-layouts  0.61 us

profile of v2, /device:TPU:0, one launch (start us, length us, event | category | flops | bytes accessed | tf_op | source)
XLA Modules:
  0.0 19.2 jit_solution(3605535338738028120)
XLA Ops:
  1.9 16.7 %tower_pair_grad.1 = f32[4,1152]{1,0:T(4,128)S(1)} custom-call(bf16[16,32,1152]{2,1,0:T(8,128)(2,1)} %tokens_hbm.1, s32[1,4]{1,0:T(1,128)} %counts_hbm.1, s32[1,16]{1,0:T(1,128)} %bitcast.2, f32[1152]{0:T(1024)} %gain_hbm.1, f32[1152]{0:T(1024)} %shift_hbm.1, bf16[1152,768]{1,0:T(8,128)(2,1)} %up_hbm.1, bf16[768,1152]{1,0:T(8,128)(2,1)} %down_hbm.1, ...), custom_call_target="tpu_custom_call" | custom-call | tf_op jit(solution)/shard_map/tower_pair_grad/pallas_call | solution.py:292
  18.6 0.6 %copy.14 = f32[4,1152]{1,0:T(4,128)} copy(f32[4,1152]{1,0:T(4,128)S(1)} %tower_pair_grad.1) | data formatting | bytes 36864
